TPU v7x, 512 devices: a whole 4x8x8 slice. The times are simulated.
512 devices in a mesh: dp: 32 (over z, y_hi), tensor: 16 (over x, y_lo, core).
Axes of the slice: x: 4, y: 8 (y_hi: 4, y_lo: 2; y = y_hi * 2 + y_lo), z: 8, core: 2. Of those that a mesh axis runs over, the one named last changes fastest.
Arguments:
- tokens_in: bfloat16 [4096, 4096], P(('dp', 'tensor')), may hold values from -6 to 6
- grad_out: bfloat16 [4096, 4096], P(('dp', 'tensor')), may hold values from -6 to 6
- gate_pre: bfloat16 [4096, 7168], P('dp', 'tensor'), may hold values from -6 to 6
- up_pre: bfloat16 [4096, 7168], P('dp', 'tensor'), may hold values from -6 to 6
- gate_weight: bfloat16 [4096, 7168], P('dp', 'tensor'), may hold values from -0.09375 to 0.09375
- up_weight: bfloat16 [4096, 7168], P('dp', 'tensor'), may hold values from -0.09375 to 0.09375
- down_weight: bfloat16 [7168, 4096], P('tensor', 'dp'), may hold values from -0.0625 to 0.0625
- norm_gain: float32 [4096], replicated, may hold values from 0.1 to 1.9
Outputs:
- input_grad: bfloat16 [4096, 4096], P(('dp', 'tensor'))
- gain_grad: float32 [4096], replicated
- down_grad: bfloat16 [7168, 4096], P('tensor', 'dp')
All inputs are finite; a program needn't handle non-finite values.
Results may differ from a plain program's by a relative error of at most 0.015.
Values may be sent and summed in bfloat16 or wider, within the bound.
A program may use at most 64 MiB of HBM per device.

v0:
```python
import jax
import jax.numpy as jnp
from jax import lax
from jax.sharding import Mesh
from jax.sharding import PartitionSpec as P

Z = "dp_0"
YH = "dp_1"
TENSOR = ("tensor_0", "tensor_1", "tensor_2")
DP = ("dp_0", "dp_1")
DP_TENSOR = ("dp_0", "dp_1", "tensor_0", "tensor_1", "tensor_2")


def nt(a, b):
    return lax.dot_general(a, b, (((1,), (1,)), ((), ())), preferred_element_type=jnp.float32)


def tn(a, b):
    return lax.dot_general(a, b, (((0,), (0,)), ((), ())), preferred_element_type=jnp.float32)


def swap(x, axis):
    return lax.all_to_all(x, axis, split_axis=0, concat_axis=0, tiled=True)


def per_device(
    tokens_in, grad_out, gate_pre, up_pre, gate_weight, up_weight, down_weight, norm_gain
):
    mine = swap(grad_out.reshape(8, 8, 4, 128).transpose(2, 0, 1, 3), YH)
    rows = lax.all_gather(mine.reshape(32, 1024), TENSOR, axis=0, tiled=True)
    rows = rows.reshape(16, 4, 8, 1024).transpose(1, 0, 2, 3).reshape(512, 1024)
    down = lax.all_gather(down_weight, Z, axis=1, tiled=True)
    gate_w = lax.all_gather(gate_weight, Z, axis=0, tiled=True)
    up_w = lax.all_gather(up_weight, Z, axis=0, tiled=True)
    gate = lax.all_gather(gate_pre, YH, axis=0, tiled=True).astype(jnp.float32)
    up = lax.all_gather(up_pre, YH, axis=0, tiled=True).astype(jnp.float32)
    sig = jax.nn.sigmoid(gate)
    silu = gate * sig
    act = (silu * up).astype(jnp.bfloat16)
    part = nt(rows, down).astype(jnp.bfloat16).reshape(4, 128, 448)
    grad_act = swap(part, YH).astype(jnp.float32).sum(axis=0).astype(jnp.bfloat16)
    grad_act = lax.all_gather(grad_act, YH, axis=0, tiled=True).astype(jnp.float32)
    grad_gate = (grad_act * up * sig * (1.0 + gate * (1.0 - sig))).astype(jnp.bfloat16)
    grad_up = (grad_act * silu).astype(jnp.bfloat16)
    norm = (nt(grad_gate, gate_w) + nt(grad_up, up_w)).astype(jnp.bfloat16)
    norm = norm.reshape(4, 16, 8, 1024).transpose(1, 0, 2, 3)
    norm = swap(norm, TENSOR).astype(jnp.float32).sum(axis=0)
    norm = swap(norm, YH).reshape(4, 8, 8, 128)
    grad_norm = norm.transpose(1, 2, 0, 3).reshape(8, 4096)
    total = tn(act, rows).astype(jnp.bfloat16).reshape(448, 8, 128).transpose(1, 0, 2)
    down_grad = swap(total, Z).astype(jnp.float32).sum(axis=0).astype(jnp.bfloat16)
    inputs = tokens_in.astype(jnp.float32)
    inv_rms = lax.rsqrt(jnp.mean(inputs * inputs, axis=1, keepdims=True) + 1e-05)
    normed = inputs * inv_rms
    gain_grad = lax.psum(jnp.sum(grad_norm * normed, axis=0), DP_TENSOR)
    scaled = grad_norm * norm_gain
    inner = jnp.mean(scaled * normed, axis=1, keepdims=True)
    input_grad = (grad_out.astype(jnp.float32) + inv_rms * (scaled - normed * inner)).astype(
        jnp.bfloat16
    )
    return (input_grad, gain_grad, down_grad)


def solution(mesh):
    finer = Mesh(
        mesh.devices.reshape(8, 4, 4, 2, 2), ("dp_0", "dp_1", "tensor_0", "tensor_1", "tensor_2")
    )
    return jax.shard_map(
        per_device,
        mesh=finer,
        in_specs=(
            P(DP_TENSOR, None),
            P(DP_TENSOR, None),
            P(DP, TENSOR),
            P(DP, TENSOR),
            P(DP, TENSOR),
            P(DP, TENSOR),
            P(TENSOR, DP),
            P(),
        ),
        out_specs=(P(DP_TENSOR, None), P(), P(TENSOR, DP)),
        check_vma=False,
    )
```

profile of v0, /device:TPU:1, one launch (start us, length us, event | category | flops | bytes accessed | tf_op | source)
XLA Modules:
  0.0 346.4 jit_solution(479711068150174751)
XLA Ops:
  7.2 0.9 copy.37
  8.1 14.3 %all_to_all.25 = bf16[4,8,8,128]{3,2,1,0:T(8,128)(2,1)S(1)} all-to-all(bf16[4,8,8,128]{3,2,1,0:T(8,128)(2,1)S(1)} %bitcast.51), channel_id=1, replica_groups=mesh['dp_0'=8,'dp_1'=4,'tensor_0'=4,'tensor_1'=2,'tensor_2'=2] {'dp_1'}, dimensions={0} | all-to-all | bytes 131072 | tf_op jit(solution)/shard_map/all_to_all | solution.py:23
  22.4 0.6 copy.36
  23.1 28.1 %all_gather.26 = bf16[1024,448]{0,1:T(8,128)(2,1)S(1)} all-gather(bf16[128,448]{0,1:T(8,128)(2,1)} %param.12), channel_id=1, replica_groups=mesh['dp_0'=8,'dp_1'=4,'tensor_0'=4,'tensor_1'=2,'tensor_2'=2] {'dp_0'}, dimensions={0}, use_global_device_ids=true | all-gather | bytes 1032192 | tf_op jit(solution)/shard_map/all_gather | solution.py:33
  51.2 22.6 %all_gather.22 = bf16[448,1024]{1,0:T(8,128)(2,1)S(1)} all-gather(bf16[448,128]{1,0:T(8,128)(2,1)} %param.14), channel_id=1, replica_groups=mesh['dp_0'=8,'dp_1'=4,'tensor_0'=4,'tensor_1'=2,'tensor_2'=2] {'dp_0'}, dimensions={1}, use_global_device_ids=true | all-gather | bytes 1032192 | tf_op jit(solution)/shard_map/all_gather | solution.py:32
  73.7 1.3 copy.17
  75.1 0.7 fusion.1
  75.8 0.8 copy.34
  76.6 3.5 all-to-all-start.1
  80.1 23.9 %all_gather.25 = bf16[512,448]{0,1:T(8,128)(2,1)S(1)} all-gather(bf16[128,448]{0,1:T(8,128)(2,1)S(1)} %copy-done.5), channel_id=1, replica_groups=mesh['dp_0'=8,'dp_1'=4,'tensor_0'=4,'tensor_1'=2,'tensor_2'=2] {'dp_1'}, dimensions={0}, use_global_device_ids=true | all-gather | bytes 573440 | tf_op jit(solution)/shard_map/all_gather | solution.py:35
  104.0 16.0 %all_gather.24 = bf16[512,448]{0,1:T(8,128)(2,1)S(1)} all-gather(bf16[128,448]{0,1:T(8,128)(2,1)S(1)} %copy-done.6), channel_id=1, replica_groups=mesh['dp_0'=8,'dp_1'=4,'tensor_0'=4,'tensor_1'=2,'tensor_2'=2] {'dp_1'}, dimensions={0}, use_global_device_ids=true | all-gather | bytes 573440 | tf_op jit(solution)/shard_map/all_gather | solution.py:36
  120.0 20.3 %all_gather.27 = bf16[1024,448]{0,1:T(8,128)(2,1)} all-gather(bf16[128,448]{0,1:T(8,128)(2,1)} %param.13), channel_id=1, replica_groups=mesh['dp_0'=8,'dp_1'=4,'tensor_0'=4,'tensor_1'=2,'tensor_2'=2] {'dp_0'}, dimensions={0}, use_global_device_ids=true | all-gather | bytes 1032192 | tf_op jit(solution)/shard_map/all_gather | solution.py:34
  140.4 16.1 %all_gather.23 = bf16[512,448]{0,1:T(8,128)(2,1)S(1)} all-gather(bf16[128,448]{0,1:T(8,128)(2,1)S(1)} %reduce_sum.61), channel_id=1, replica_groups=mesh['dp_0'=8,'dp_1'=4,'tensor_0'=4,'tensor_1'=2,'tensor_2'=2] {'dp_1'}, dimensions={0}, use_global_device_ids=true | all-gather | bytes 573440 | tf_op jit(solution)/shard_map/all_gather | solution.py:42
  156.6 0.9 fusion.11
  157.5 0.2 copy-done
  157.8 0.8 add_convert_fusion
  158.6 1.1 copy.32
  159.7 25.8 %all-to-all-start.2 = ((bf16[16,4,8,1024]{3,2,1,0:T(8,128)(2,1)}), bf16[16,4,8,1024]{3,2,1,0:T(8,128)(2,1)S(1)}, u32[]{:S(2)}, u32[]{:S(2)}) async-start(bf16[16,4,8,1024]{3,2,1,0:T(8,128)(2,1)} %bitcast.36), calls=%async_computation.2 | async-start | bytes 2097152 | tf_op jit(solution)/shard_map/all_to_all | solution.py:23
  185.5 0.7 fusion
  186.2 1.1 copy.33
  187.4 13.8 %all-to-all-done.2 = bf16[16,4,8,1024]{3,2,1,0:T(8,128)(2,1)S(1)} async-done(((bf16[16,4,8,1024]{3,2,1,0:T(8,128)(2,1)}), bf16[16,4,8,1024]{3,2,1,0:T(8,128)(2,1)S(1)}, u32[]{:S(2)}, u32[]{:S(2)}) %all-to-all-start.2) | async-done | bytes 1048608 | tf_op jit(solution)/shard_map/all_to_all | solution.py:23
  201.1 4.5 %all-to-all-start.4 = ((bf16[8,448,128]{2,1,0:T(8,128)(2,1)}), bf16[8,448,128]{2,1,0:T(8,128)(2,1)S(1)}, u32[]{:S(2)}, u32[]{:S(2)}) async-start(bf16[8,448,128]{2,1,0:T(8,128)(2,1)} %bitcast.38), calls=%async_computation.4 | async-start | bytes 1835008 | tf_op jit(solution)/shard_map/all_to_all | solution.py:23
  205.6 0.1 fusion.25
  205.8 0.8 convert_reduce_fusion
  206.6 25.4 %all-to-all-done.4 = bf16[8,448,128]{2,1,0:T(8,128)(2,1)S(1)} async-done(((bf16[8,448,128]{2,1,0:T(8,128)(2,1)}), bf16[8,448,128]{2,1,0:T(8,128)(2,1)S(1)}, u32[]{:S(2)}, u32[]{:S(2)}) %all-to-all-start.4) | async-done | bytes 917536 | tf_op jit(solution)/shard_map/all_to_all | solution.py:23
  232.0 4.0 %all-to-all-start.3 = ((f32[4,8,1024]{2,1,0:T(8,128)}), f32[4,8,1024]{2,1,0:T(8,128)S(1)}, u32[]{:S(2)}, u32[]{:S(2)}) async-start(f32[4,8,1024]{2,1,0:T(8,128)} %convert_reduce_fusion), calls=%async_computation.3 | async-start | bytes 262144 | tf_op jit(solution)/shard_map/all_to_all | solution.py:23
  236.0 0.8 reduce_sum.65
  236.8 6.6 %all-to-all-done.3 = f32[4,8,1024]{2,1,0:T(8,128)S(1)} async-done(((f32[4,8,1024]{2,1,0:T(8,128)}), f32[4,8,1024]{2,1,0:T(8,128)S(1)}, u32[]{:S(2)}, u32[]{:S(2)}) %all-to-all-start.3) | async-done | bytes 131104 | tf_op jit(solution)/shard_map/all_to_all | solution.py:23
  243.4 0.1 copy.20
  243.6 0.2 fusion.24
  243.8 95.1 %psum.7 = f32[4096]{0:T(1024)} all-reduce(f32[4096]{0:T(1024)S(1)} %get-tuple-element.3), channel_id=1, replica_groups=mesh['dp_0'=8,'dp_1'=4,'tensor_0'=4,'tensor_1'=2,'tensor_2'=2] {'dp_0','..., use_global_device_ids=true, to_apply=%region_5.0 | all-reduce | flops 4096 | bytes 32768 | tf_op jit(solution)/shard_map/psum | solution.py:55
  338.9 0.7 fusion.23
  (24 shorter events, 0.3 us)
Async XLA Ops:
  7.2 66.6 %all-gather.2.cloned.1.call-start = ((), (), s32[]{:S(2)}) async-start(), calls=%async_computation.5 | async-start | bytes 1114112 | tf_op jit(solution)/shard_map/all_gather | solution.py:30
  75.1 5.0 %copy-start.5 = (bf16[128,448]{0,1:T(8,128)(2,1)S(1)}, bf16[128,448]{0,1:T(8,128)(2,1)}, u32[]{:S(2)}) copy-start(bf16[128,448]{0,1:T(8,128)(2,1)} %param.10) | copy-start | bytes 344068
  75.7 28.2 %copy-start.6 = (bf16[128,448]{0,1:T(8,128)(2,1)S(1)}, bf16[128,448]{0,1:T(8,128)(2,1)}, u32[]{:S(2)}) copy-start(bf16[128,448]{0,1:T(8,128)(2,1)} %param.11) | copy-start | bytes 344068
  76.6 63.8 %all-to-all-start.1 = ((bf16[4,128,448]{1,2,0:T(8,128)(2,1)}), bf16[4,128,448]{1,2,0:T(8,128)(2,1)S(1)}, u32[]{:S(2)}, u32[]{:S(2)}) async-start(bf16[4,128,448]{1,2,0:T(8,128)(2,1)} %bitcast.39), calls=%async_computation.1 | async-start | bytes 917504 | tf_op jit(solution)/shard_map/all_to_all | solution.py:23
  120.0 37.5 %copy-start.2 = (bf16[512,448]{0,1:T(8,128)(2,1)}, bf16[512,448]{0,1:T(8,128)(2,1)S(1)}, u32[]{:S(2)}) copy-start(bf16[512,448]{0,1:T(8,128)(2,1)S(1)} %all_gather.24) | copy-start | bytes 1376260
  156.6 1.2 copy-start
  158.6 26.9 %copy-start.3 = (bf16[512,448]{0,1:T(8,128)(2,1)S(1)}, bf16[512,448]{0,1:T(8,128)(2,1)}, u32[]{:S(2)}) copy-start(bf16[512,448]{0,1:T(8,128)(2,1)} %copy-done.2) | copy-start | bytes 1376260
  159.7 41.5 %all-to-all-start.2 = ((bf16[16,4,8,1024]{3,2,1,0:T(8,128)(2,1)}), bf16[16,4,8,1024]{3,2,1,0:T(8,128)(2,1)S(1)}, u32[]{:S(2)}, u32[]{:S(2)}) async-start(bf16[16,4,8,1024]{3,2,1,0:T(8,128)(2,1)} %bitcast.36), calls=%async_computation.2 | async-start | bytes 2097152 | tf_op jit(solution)/shard_map/all_to_all | solution.py:23
  186.2 19.4 %copy-start.1 = (bf16[8,4096]{1,0:T(8,128)(2,1)S(1)}, bf16[8,4096]{1,0:T(8,128)(2,1)}, u32[]{:S(2)}) copy-start(bf16[8,4096]{1,0:T(8,128)(2,1)} %param.8) | copy-start | bytes 196612
  201.1 30.9 %all-to-all-start.4 = ((bf16[8,448,128]{2,1,0:T(8,128)(2,1)}), bf16[8,448,128]{2,1,0:T(8,128)(2,1)S(1)}, u32[]{:S(2)}, u32[]{:S(2)}) async-start(bf16[8,448,128]{2,1,0:T(8,128)(2,1)} %bitcast.38), calls=%async_computation.4 | async-start | bytes 1835008 | tf_op jit(solution)/shard_map/all_to_all | solution.py:23
  205.6 37.9 %copy-start.7 = (f32[4096]{0:T(1024)S(1)}, f32[4096]{0:T(1024)}, u32[]{:S(2)}) copy-start(f32[4096]{0:T(1024)} %param.15) | copy-start | bytes 49156
  205.6 133.2 %copy-start.4 = (bf16[8,4096]{1,0:T(8,128)(2,1)S(1)}, bf16[8,4096]{1,0:T(8,128)(2,1)}, u32[]{:S(2)}) copy-start(bf16[8,4096]{1,0:T(8,128)(2,1)} %param.9) | copy-start | bytes 196612
  232.0 11.4 %all-to-all-start.3 = ((f32[4,8,1024]{2,1,0:T(8,128)}), f32[4,8,1024]{2,1,0:T(8,128)S(1)}, u32[]{:S(2)}, u32[]{:S(2)}) async-start(f32[4,8,1024]{2,1,0:T(8,128)} %convert_reduce_fusion), calls=%async_computation.3 | async-start | bytes 262144 | tf_op jit(solution)/shard_map/all_to_all | solution.py:23
Sparse Core Ops, SparseCore 0:
  23.2 39.1 all-gather.1
where the time goes:
time: 347 us; the launch traced here: 346 us
  blocking collectives  236 us (68%)
  waiting for transfers between devices  45.7 us (13%)
  starting transfers between devices  37.8 us (11%)
  between operations  14.2 us (4%)
  local copies, waits for them, and re-layouts  6.3 us (2%)
    psum x1, blocking collectives, per_device(): gain_grad = lax.psum(jnp.sum(grad_norm * normed, axis=0), DP_TENSOR)  95.1 us
    all_to_all x4, waiting for transfers between devices, swap(): return lax.all_to_all(x, axis, split_axis=0, concat_axis=0, tiled=True)  45.7 us
    all_to_all x4, starting transfers between devices, swap(): return lax.all_to_all(x, axis, split_axis=0, concat_axis=0, tiled=True)  37.8 us
    all_gather x1, blocking collectives, per_device(): gate_w = lax.all_gather(gate_weight, Z, axis=0, tiled=True)  28.1 us
    all_gather x1, blocking collectives, per_device(): gate = lax.all_gather(gate_pre, YH, axis=0, tiled=True).astype(jnp.float32)  23.9 us
    all_gather x1, blocking collectives, per_device(): down = lax.all_gather(down_weight, Z, axis=1, tiled=True)  22.6 us
    all_gather x1, blocking collectives, per_device(): up_w = lax.all_gather(up_weight, Z, axis=0, tiled=True)  20.3 us
    all_gather x1, blocking collectives, per_device(): lax.all_gather(grad_act, YH, axis=0, tiled=True).astype(jnp.float32)  16.1 us
  transfers between devices with their start and end apart: 5, of which 3 were waited for; matrix products, arithmetic and copies ran while one was open for 1% of the time, Pallas kernels for 0%

commit v1 on v0

--- a/solution.py
+++ b/solution.py
@@ -9,6 +9,11 @@
 TENSOR = ("tensor_0", "tensor_1", "tensor_2")
 DP = ("dp_0", "dp_1")
 DP_TENSOR = ("dp_0", "dp_1", "tensor_0", "tensor_1", "tensor_2")
+
+
+def perform_the_arrays(frame, lane_axis):
+    outer = lax.all_gather(frame, lane_axis).sum(axis=0)
+    return outer
 
 
 def nt(a, b):
@@ -52,7 +57,7 @@
     inputs = tokens_in.astype(jnp.float32)
     inv_rms = lax.rsqrt(jnp.mean(inputs * inputs, axis=1, keepdims=True) + 1e-05)
     normed = inputs * inv_rms
-    gain_grad = lax.psum(jnp.sum(grad_norm * normed, axis=0), DP_TENSOR)
+    gain_grad = perform_the_arrays(jnp.sum(grad_norm * normed, axis=0), DP_TENSOR)
     scaled = grad_norm * norm_gain
     inner = jnp.mean(scaled * normed, axis=1, keepdims=True)
     input_grad = (grad_out.astype(jnp.float32) + inv_rms * (scaled - normed * inner)).astype(

time: 347 us -> 1060 us (3.05)
  waiting for transfers between devices: 45.7 us -> 809 us
  blocking collectives: 236 us -> 169 us
    all_gather x0 -> x1, waiting for transfers between devices: none -> 786 us  [perform_the_arrays(): outer = lax.all_gather(frame, lane_axis).sum(axis=0)]
    psum x1 -> x0, blocking collectives: 95.1 us -> none  [per_device(): gain_grad = lax.psum(jnp.sum(grad_norm * normed, axis=0), DP_TENSOR)]
    all_to_all x1 -> x2, blocking collectives: 14.3 us -> 41.6 us  [swap(): return lax.all_to_all(x, axis, split_axis=0, concat_axis=0, tiled=True)]
    all_to_all x4 -> x3, waiting for transfers between devices: 45.7 us -> 22.8 us  [swap(): return lax.all_to_all(x, axis, split_axis=0, concat_axis=0, tiled=True)]
    all_to_all x4 -> x3, starting transfers between devices: 37.8 us -> 32.9 us  [swap(): return lax.all_to_all(x, axis, split_axis=0, concat_axis=0, tiled=True)]
  transfers between devices with their start and end apart: 5 -> 5, of which waited for: 3 -> 3; matrix products, arithmetic and copies ran while one was open for 1% -> 0% of each run, Pallas kernels for 0% -> 0%
where the time goes in v1:
time: 1060 us; the launch traced here: 1050 us
  waiting for transfers between devices  809 us (76%)
  blocking collectives  169 us (16%)
  starting transfers between devices  33 us (3%)
  local copies, waits for them, and re-layouts  14.7 us (1%)
  between operations  14.2 us (1%)
    all_gather x1, waiting for transfers between devices, perform_the_arrays(): outer = lax.all_gather(frame, lane_axis).sum(axis=0)  786 us
    all_to_all x2, blocking collectives, swap(): return lax.all_to_all(x, axis, split_axis=0, concat_axis=0, tiled=True)  41.6 us
    all_to_all x3, starting transfers between devices, swap(): return lax.all_to_all(x, axis, split_axis=0, concat_axis=0, tiled=True)  32.9 us
    all_gather x1, blocking collectives, per_device(): gate_w = lax.all_gather(gate_weight, Z, axis=0, tiled=True)  28.1 us
    all_gather x1, blocking collectives, per_device(): gate = lax.all_gather(gate_pre, YH, axis=0, tiled=True).astype(jnp.float32)  23.9 us
    all_to_all x3, waiting for transfers between devices, swap(): return lax.all_to_all(x, axis, split_axis=0, concat_axis=0, tiled=True)  22.8 us
    all_gather x1, blocking collectives, per_device(): down = lax.all_gather(down_weight, Z, axis=1, tiled=True)  22.6 us
  transfers between devices with their start and end apart: 5, of which 3 were waited for; matrix products, arithmetic and copies ran while one was open for 0% of the time, Pallas kernels for 0%

profile of v1, /device:TPU:1, one launch (start us, length us, event | category | flops | bytes accessed | tf_op | source)
XLA Modules:
  0.0 1050.7 jit_solution(15447620080094260078)
XLA Ops:
  7.2 0.9 copy.43
  8.1 14.3 %all_to_all.25 = bf16[4,8,8,128]{3,2,1,0:T(8,128)(2,1)S(1)} all-to-all(bf16[4,8,8,128]{3,2,1,0:T(8,128)(2,1)S(1)} %bitcast.52), channel_id=1, replica_groups=mesh['dp_0'=8,'dp_1'=4,'tensor_0'=4,'tensor_1'=2,'tensor_2'=2] {'dp_1'}, dimensions={0} | all-to-all | bytes 131072 | tf_op jit(solution)/shard_map/all_to_all | solution.py:28
  22.4 0.6 copy.42
  23.1 28.1 %all_gather.32 = bf16[1024,448]{0,1:T(8,128)(2,1)S(1)} all-gather(bf16[128,448]{0,1:T(8,128)(2,1)} %param.12), channel_id=1, replica_groups=mesh['dp_0'=8,'dp_1'=4,'tensor_0'=4,'tensor_1'=2,'tensor_2'=2] {'dp_0'}, dimensions={0}, use_global_device_ids=true | all-gather | bytes 1032192 | tf_op jit(solution)/shard_map/all_gather | solution.py:38
  51.2 22.6 %all_gather.28 = bf16[448,1024]{1,0:T(8,128)(2,1)S(1)} all-gather(bf16[448,128]{1,0:T(8,128)(2,1)} %param.14), channel_id=1, replica_groups=mesh['dp_0'=8,'dp_1'=4,'tensor_0'=4,'tensor_1'=2,'tensor_2'=2] {'dp_0'}, dimensions={1}, use_global_device_ids=true | all-gather | bytes 1032192 | tf_op jit(solution)/shard_map/all_gather | solution.py:37
  73.7 1.3 copy.23
  75.1 0.7 fusion.1
  75.8 0.9 copy.40
  76.6 3.5 all-to-all-start.1
  80.1 23.9 %all_gather.31 = bf16[512,448]{0,1:T(8,128)(2,1)S(1)} all-gather(bf16[128,448]{0,1:T(8,128)(2,1)S(1)} %copy-done.5), channel_id=1, replica_groups=mesh['dp_0'=8,'dp_1'=4,'tensor_0'=4,'tensor_1'=2,'tensor_2'=2] {'dp_1'}, dimensions={0}, use_global_device_ids=true | all-gather | bytes 573440 | tf_op jit(solution)/shard_map/all_gather | solution.py:40
  104.0 16.1 %all_gather.30 = bf16[512,448]{0,1:T(8,128)(2,1)S(1)} all-gather(bf16[128,448]{0,1:T(8,128)(2,1)S(1)} %copy-done.6), channel_id=1, replica_groups=mesh['dp_0'=8,'dp_1'=4,'tensor_0'=4,'tensor_1'=2,'tensor_2'=2] {'dp_1'}, dimensions={0}, use_global_device_ids=true | all-gather | bytes 573440 | tf_op jit(solution)/shard_map/all_gather | solution.py:41
  120.1 20.3 %all_gather.33 = bf16[1024,448]{0,1:T(8,128)(2,1)} all-gather(bf16[128,448]{0,1:T(8,128)(2,1)} %param.13), channel_id=1, replica_groups=mesh['dp_0'=8,'dp_1'=4,'tensor_0'=4,'tensor_1'=2,'tensor_2'=2] {'dp_0'}, dimensions={0}, use_global_device_ids=true | all-gather | bytes 1032192 | tf_op jit(solution)/shard_map/all_gather | solution.py:39
  140.4 16.6 %all_gather.29 = bf16[512,448]{0,1:T(8,128)(2,1)S(1)} all-gather(bf16[128,448]{0,1:T(8,128)(2,1)S(1)} %reduce_sum.70), channel_id=1, replica_groups=mesh['dp_0'=8,'dp_1'=4,'tensor_0'=4,'tensor_1'=2,'tensor_2'=2] {'dp_1'}, dimensions={0}, use_global_device_ids=true | all-gather | bytes 573440 | tf_op jit(solution)/shard_map/all_gather | solution.py:47
  157.0 0.9 fusion.11
  158.0 0.2 copy-done
  158.2 0.8 add_convert_fusion
  159.0 1.1 copy.38
  160.1 25.9 %all-to-all-start.2 = ((bf16[16,4,8,1024]{3,2,1,0:T(8,128)(2,1)}), bf16[16,4,8,1024]{3,2,1,0:T(8,128)(2,1)S(1)}, u32[]{:S(2)}, u32[]{:S(2)}) async-start(bf16[16,4,8,1024]{3,2,1,0:T(8,128)(2,1)} %bitcast.36), calls=%async_computation.2 | async-start | bytes 2097152 | tf_op jit(solution)/shard_map/all_to_all | solution.py:28
  186.1 0.1 fusion.25
  186.2 15.5 %all-to-all-done.2 = bf16[16,4,8,1024]{3,2,1,0:T(8,128)(2,1)S(1)} async-done(((bf16[16,4,8,1024]{3,2,1,0:T(8,128)(2,1)}), bf16[16,4,8,1024]{3,2,1,0:T(8,128)(2,1)S(1)}, u32[]{:S(2)}, u32[]{:S(2)}) %all-to-all-start.2) | async-done | bytes 1048608 | tf_op jit(solution)/shard_map/all_to_all | solution.py:28
  201.7 0.8 convert_reduce_fusion
  202.6 3.5 all-to-all-start.3
  206.1 7.3 all-to-all-done.3
  213.7 0.7 fusion.24
  214.4 0.7 fusion
  215.2 0.2 copy.39
  215.3 27.3 %all_to_all.26 = bf16[8,448,128]{2,1,0:T(8,128)(2,1)S(1)} all-to-all(bf16[8,448,128]{2,1,0:T(8,128)(2,1)S(1)} %bitcast.44), channel_id=1, replica_groups=mesh['dp_0'=8,'dp_1'=4,'tensor_0'=4,'tensor_1'=2,'tensor_2'=2] {'dp_0'}, dimensions={0} | all-to-all | bytes 1835008 | tf_op jit(solution)/shard_map/all_to_all | solution.py:28
  242.6 0.8 reduce_sum.75
  243.4 0.7 fusion.23
  244.2 785.9 %all-gather.6.cloned.1.call-done = f32[2097152]{0:T(1024)} async-done(((f32[4096]{0:T(1024)}), f32[2097152]{0:T(1024)}) %all-gather.6.cloned.1.call-update) | async-done | bytes 8388624 | tf_op jit(solution)/shard_map/all_gather | solution.py:15
  1030.1 9.4 reshape.55
  1039.5 4.4 reduce_sum.74
  (27 shorter events, 0.4 us)
Async XLA Ops:
  7.2 66.6 %all-gather.4.cloned.1.call-start = ((), (), s32[]{:S(2)}) async-start(), calls=%async_computation.5 | async-start | bytes 1114112 | tf_op jit(solution)/shard_map/all_gather | solution.py:35
  75.1 5.0 copy-start.5
  75.7 28.2 %copy-start.6 = (bf16[128,448]{0,1:T(8,128)(2,1)S(1)}, bf16[128,448]{0,1:T(8,128)(2,1)}, u32[]{:S(2)}) copy-start(bf16[128,448]{0,1:T(8,128)(2,1)} %param.11) | copy-start | bytes 344068
  76.6 63.7 %all-to-all-start.1 = ((bf16[4,128,448]{1,2,0:T(8,128)(2,1)}), bf16[4,128,448]{1,2,0:T(8,128)(2,1)S(1)}, u32[]{:S(2)}, u32[]{:S(2)}) async-start(bf16[4,128,448]{1,2,0:T(8,128)(2,1)} %bitcast.39), calls=%async_computation.1 | async-start | bytes 917504 | tf_op jit(solution)/shard_map/all_to_all | solution.py:28
  120.1 37.9 %copy-start.2 = (bf16[512,448]{0,1:T(8,128)(2,1)}, bf16[512,448]{0,1:T(8,128)(2,1)S(1)}, u32[]{:S(2)}) copy-start(bf16[512,448]{0,1:T(8,128)(2,1)S(1)} %all_gather.30) | copy-start | bytes 1376260
  157.0 1.2 copy-start
  159.0 27.0 %copy-start.1 = (bf16[8,4096]{1,0:T(8,128)(2,1)S(1)}, bf16[8,4096]{1,0:T(8,128)(2,1)}, u32[]{:S(2)}) copy-start(bf16[8,4096]{1,0:T(8,128)(2,1)} %param.8) | copy-start | bytes 196612
  160.1 53.5 %copy-start.7 = (f32[4096]{0:T(1024)S(1)}, f32[4096]{0:T(1024)}, u32[]{:S(2)}) copy-start(f32[4096]{0:T(1024)} %param.15) | copy-start | bytes 49156
  160.1 54.3 %copy-start.3 = (bf16[512,448]{0,1:T(8,128)(2,1)S(1)}, bf16[512,448]{0,1:T(8,128)(2,1)}, u32[]{:S(2)}) copy-start(bf16[512,448]{0,1:T(8,128)(2,1)} %copy-done.2) | copy-start | bytes 1376260
  160.1 41.6 %all-to-all-start.2 = ((bf16[16,4,8,1024]{3,2,1,0:T(8,128)(2,1)}), bf16[16,4,8,1024]{3,2,1,0:T(8,128)(2,1)S(1)}, u32[]{:S(2)}, u32[]{:S(2)}) async-start(bf16[16,4,8,1024]{3,2,1,0:T(8,128)(2,1)} %bitcast.36), calls=%async_computation.2 | async-start | bytes 2097152 | tf_op jit(solution)/shard_map/all_to_all | solution.py:28
  202.6 10.9 %all-to-all-start.3 = ((f32[4,8,1024]{2,1,0:T(8,128)}), f32[4,8,1024]{2,1,0:T(8,128)S(1)}, u32[]{:S(2)}, u32[]{:S(2)}) async-start(f32[4,8,1024]{2,1,0:T(8,128)} %convert_reduce_fusion), calls=%async_computation.3 | async-start | bytes 262144 | tf_op jit(solution)/shard_map/all_to_all | solution.py:28
  206.1 824.0 %all-gather.6.cloned.1.call-start = ((), (), s32[]{:S(2)}) async-start(), calls=%async_computation.6 | async-start | bytes 8404992 | tf_op jit(solution)/shard_map/all_gather | solution.py:15
  215.2 28.3 %copy-start.4 = (bf16[8,4096]{1,0:T(8,128)(2,1)S(1)}, bf16[8,4096]{1,0:T(8,128)(2,1)}, u32[]{:S(2)}) copy-start(bf16[8,4096]{1,0:T(8,128)(2,1)} %param.9) | copy-start | bytes 196612
Sparse Core Ops, SparseCore 0:
  23.2 39.1 all-gather.3
  214.5 815.5 all-gather.5
